TPU v7x, 32 devices: a whole 2x2x4 slice. The times are simulated.
32 devices in a mesh: seq: 8 (over z, y), head: 4 (over x, core).
Axes of the slice: x: 2, y: 2, z: 4, core: 2. Of those that a mesh axis runs over, the one named last changes fastest.
Arguments:
- queries: bfloat16 [1024, 1536], P('seq', 'head'), may hold values from -400 to 400
- latent: bfloat16 [1024, 320], P(('seq', 'head')), may hold values from -6 to 6
- w_kv_up: bfloat16 [256, 2048], P(None, 'head'), may hold values from -0.375 to 0.375
Outputs:
- attended: bfloat16 [1024, 1024], P('seq', 'head')
All inputs are finite; a program needn't handle non-finite values.
Results may differ from a plain program's by a relative error of at most 0.004.
Values may be sent and summed in bfloat16 or wider, within the bound.
A program may use at most 64 MiB of HBM per device.

v0:
```python
import math
import jax
import jax.numpy as jnp
from jax import lax
from jax.sharding import PartitionSpec as P

D_LATENT = 256
ROPE = 64
NOPE = 128
VDIM = 128
MASKED = -1e30


def from_behind(shard, axis, by):
    length = lax.axis_size(axis)
    pairs = [(i, i + by) for i in range(length) if 0 <= i + by < length]
    return lax.ppermute(shard, axis, pairs)


def attend(state, key_block, key_start, setup):
    query_side, query_rope, query_pos, w_kv_up, absorb = setup
    numerator, running_max, totals = state
    local_heads = query_rope.shape[1]
    key_count = key_block.shape[0]
    highest = lax.Precision.HIGHEST
    key_latent = key_block[:, :D_LATENT]
    key_rope = key_block[:, D_LATENT:]
    key_value = jnp.dot(key_latent, w_kv_up, preferred_element_type=jnp.float32)
    key_value = key_value.reshape(key_count, local_heads, NOPE + VDIM)
    scores = jnp.einsum("qhd,khd->hqk", query_side, key_value[:, :, :NOPE], precision=highest)
    scores = scores + jnp.einsum(
        "qhd,kd->hqk", query_rope, key_rope, preferred_element_type=jnp.float32
    )
    scores = scores * (NOPE + ROPE) ** (-0.5)
    key_pos = key_start + lax.iota(jnp.int32, key_count)
    allowed = (key_pos[None, :] <= query_pos[:, None]) & (key_pos[None, :] >= 0)
    scores = jnp.where(allowed[None], scores, MASKED)
    new_max = jnp.maximum(running_max, jnp.max(scores, axis=2))
    factor = jnp.exp(running_max - new_max)
    weights = jnp.where(allowed[None], jnp.exp(scores - new_max[:, :, None]), 0.0)
    totals = totals * factor + jnp.sum(weights, axis=2)
    rounded = weights.astype(jnp.bfloat16)
    update = jnp.einsum(
        "hqk,khd->hqd", rounded.astype(jnp.float32), key_value[:, :, NOPE:], precision=highest
    )
    numerator = numerator * factor[:, :, None] + update
    return (numerator, new_max, totals)


def attend_blocks(state, keys, key_start, setup):
    key_total = keys.shape[0]
    block_rows = key_total if key_total <= 1024 else math.gcd(key_total, 1024)
    block_count = key_total // block_rows

    def one_block(block_index, inner):
        offset = block_index * block_rows
        piece = lax.dynamic_slice_in_dim(keys, offset, block_rows, 0)
        return attend(inner, piece, key_start + offset, setup)

    if block_count == 1:
        return one_block(0, state)
    return lax.fori_loop(0, block_count, one_block, state)


def prepare(query_rows, query_pos, w_kv_up):
    row_count = query_rows.shape[0]
    local_heads = w_kv_up.shape[1] // (NOPE + VDIM)
    query_all = query_rows.reshape(row_count, local_heads, NOPE + ROPE)
    query_side = query_all[:, :, :NOPE].astype(jnp.float32)
    width = VDIM
    setup = (query_side, query_all[:, :, NOPE:], query_pos, w_kv_up, False)
    start_state = (
        jnp.zeros((local_heads, row_count, width), jnp.float32),
        jnp.full((local_heads, row_count), MASKED, jnp.float32),
        jnp.zeros((local_heads, row_count), jnp.float32),
    )
    return (setup, start_state)


def finish(state, w_kv_up):
    numerator, running_max, totals = state
    local_heads = w_kv_up.shape[1] // (NOPE + VDIM)
    row_count = totals.shape[1]
    result = numerator / totals[:, :, None]
    return (
        jnp.transpose(result, (1, 0, 2)).reshape(row_count, local_heads * VDIM).astype(jnp.bfloat16)
    )


def body(queries, latent, w_kv_up):
    group_rows = queries.shape[0]
    seq_groups = lax.axis_size("seq")
    group_index = lax.axis_index("seq")
    query_pos = group_index * group_rows + lax.iota(jnp.int32, group_rows)
    setup, state = prepare(queries, query_pos, w_kv_up)
    gathered = lax.all_gather(latent, "head", axis=0, tiled=True)
    state = attend(state, gathered, group_index * group_rows, setup)
    history = gathered
    span_groups = 1
    while span_groups < seq_groups:
        arrived = from_behind(history, "seq", span_groups)
        state = attend_blocks(
            state, arrived, (group_index - 2 * span_groups + 1) * group_rows, setup
        )
        if 2 * span_groups < seq_groups:
            history = jnp.concatenate([arrived, history], axis=0)
        span_groups = span_groups * 2
    return finish(state, w_kv_up)


def solution(mesh):
    in_specs = (P("seq", "head"), P(("seq", "head"), None), P(None, "head"))
    out_specs = P("seq", "head")
    return jax.shard_map(body, mesh=mesh, in_specs=in_specs, out_specs=out_specs, check_vma=False)
```

profile of v0, /device:TPU:27, one launch (start us, length us, event | category | flops | bytes accessed | tf_op | source)
XLA Modules:
  0.0 42.7 jit_solution(3402798072797051808)
XLA Ops:
  0.0 0.0 copy-start
  0.0 6.2 %all_gather.3 = bf16[128,320]{1,0:T(8,128)(2,1)S(1)} all-gather(bf16[32,320]{1,0:T(8,128)(2,1)} %param.4), channel_id=1, replica_groups=mesh['seq'=8,'head'=4] {'head'}, dimensions={0}, use_global_device_ids=true | all-gather | bytes 102400 | tf_op jit(solution)/shard_map/all_gather | solution.py:96
  6.2 0.0 copy-start.1
  6.2 0.1 copy.39
  6.3 3.1 %collective-permute-start = (bf16[128,320]{0,1:T(8,128)(2,1)S(1)}, bf16[128,320]{0,1:T(8,128)(2,1)S(1)}, u32[]{:S(2)}, u32[]{:S(2)}) collective-permute-start(bf16[128,320]{0,1:T(8,128)(2,1)S(1)} %copy.39), channel_id=1, source_target_pairs={{0,4},{4,8},{8,12},{12,16},{16,20},{20,24},{24,28},{1,5},{5,9},{9,... | collective-permute-start | bytes 245768 | tf_op jit(solution)/shard_map/ppermute | solution.py:17
  9.6 0.0 copy-done.1
  9.6 0.1 copy.37
  9.7 0.2 convolution_bitcast_fusion.11
  9.9 0.0 copy-done
  9.9 0.2 fusion.53
  10.1 0.2 reshape.297
  10.3 0.1 fusion.86
  10.4 0.2 compare_and_fusion
  10.6 0.1 compare_and_fusion.2
  10.7 0.2 fusion.90
  10.9 0.1 compare_and_fusion.1
  11.1 1.8 %collective-permute-done = bf16[128,320]{0,1:T(8,128)(2,1)S(1)} collective-permute-done((bf16[128,320]{0,1:T(8,128)(2,1)S(1)}, bf16[128,320]{0,1:T(8,128)(2,1)S(1)}, u32[]{:S(2)}, u32[]{:S(2)}) %collective-permute-start) | collective-permute-done | bytes 81952 | tf_op jit(solution)/shard_map/ppermute | solution.py:17
  12.9 1.3 %collective-permute-start.1 = (bf16[256,320]{0,1:T(8,128)(2,1)S(1)}, bf16[256,320]{0,1:T(8,128)(2,1)S(1)}, u32[]{:S(2)}, u32[]{:S(2)}) collective-permute-start(bf16[256,320]{0,1:T(8,128)(2,1)S(1)} %pad_maximum_fusion.1), channel_id=1, source_target_pairs={{0,8},{4,12},{8,16},{12,20},{16,24},{20,28},{1,9},{5,13},{9,17},{1... | collective-permute-start | bytes 491528 | tf_op jit(solution)/shard_map/ppermute | solution.py:17
  14.2 0.2 fusion.51
  14.5 0.2 reshape.299
  14.6 0.1 fusion.85
  14.7 0.2 convolution_bitcast_fusion.7
  14.9 0.2 fusion.89
  15.2 4.4 %collective-permute-done.1 = bf16[256,320]{0,1:T(8,128)(2,1)S(1)} collective-permute-done((bf16[256,320]{0,1:T(8,128)(2,1)S(1)}, bf16[256,320]{0,1:T(8,128)(2,1)S(1)}, u32[]{:S(2)}, u32[]{:S(2)}) %collective-permute-start.1) | collective-permute-done | bytes 163872 | tf_op jit(solution)/shard_map/ppermute | solution.py:17
  19.6 1.3 %collective-permute-start.2 = (bf16[512,320]{0,1:T(8,128)(2,1)S(1)}, bf16[512,320]{0,1:T(8,128)(2,1)S(1)}, u32[]{:S(2)}, u32[]{:S(2)}) collective-permute-start(bf16[512,320]{0,1:T(8,128)(2,1)S(1)} %pad_maximum_fusion), channel_id=1, source_target_pairs={{0,16},{4,20},{8,24},{12,28},{1,17},{5,21},{9,25},{13,29},{2,18},{... | collective-permute-start | bytes 983048 | tf_op jit(solution)/shard_map/ppermute | solution.py:17
  20.9 0.2 fusion.36
  21.2 0.3 reshape.300
  21.5 0.2 fusion.84
  21.7 0.2 convolution_bitcast_fusion.2
  21.9 0.2 fusion.88
  22.2 16.7 %collective-permute-done.2 = bf16[512,320]{0,1:T(8,128)(2,1)S(1)} collective-permute-done((bf16[512,320]{0,1:T(8,128)(2,1)S(1)}, bf16[512,320]{0,1:T(8,128)(2,1)S(1)}, u32[]{:S(2)}, u32[]{:S(2)}) %collective-permute-start.2) | collective-permute-done | bytes 327712 | tf_op jit(solution)/shard_map/ppermute | solution.py:17
  38.9 0.3 fusion.26
  39.3 0.6 %convolution_bitcast_fusion.1 = f32[2,128,512]{1,2,0:T(8,128)S(1)} fusion(f32[512,2,256]{0,2,1:T(8,128)S(1)} %bitcast.164, bf16[128,2,192]{0,2,1:T(8,128)(2,1)S(1)} %bitcast.162), kind=kOutput, calls=%fused_computation.2 | convolution fusion | flops 201326592 | bytes 1114112 | tf_op jit(solution)/shard_map/qhd,khd->hqk/dot_general | solution.py:30
  39.9 0.3 fusion.87
  40.2 0.1 fusion.23
  40.3 0.1 fusion.33
  40.4 0.1 fusion.45
  40.5 0.3 fusion.15
  40.8 0.3 fusion.16
  41.1 0.4 %fusion.9 = f32[128,2,128]{0,2,1:T(8,128)S(1)} fusion(f32[128,2,128]{0,2,1:T(8,128)S(1)} %fusion.16, f32[256,2,128]{2,1,0:T(2,128)S(1)} %get-tuple-element.11, f32[2,128,256]{1,2,0:T(8,128)S(1)} %get-tuple-element.25, f32[2,128]{1,0:T(2,128)S(1)} %get-tuple-element.9, pred[128,256]{0,1:T(8,128)(4,1)S(1)} %compare_and_fusion.1, ...), kind=kOutput, calls=%fused_computation.15 | convolution fusion | flops 100925440 | bytes 821248 | tf_op jit(solution)/shard_map/hqk,khd->hqd/dot_general | solution.py:43
  41.5 0.4 %fusion.20 = bf16[128,2,128]{0,2,1:T(8,128)(2,1)S(1)} fusion(f32[128,2,128]{0,2,1:T(8,128)S(1)} %fusion.9, f32[512,2,256]{0,2,1:T(8,128)S(1)} %bitcast.165, f32[2,128,512]{1,2,0:T(8,128)S(1)} %get-tuple-element.23, f32[2,128]{1,0:T(2,128)S(1)} %get-tuple-element.8, pred[128,512]{0,1:T(8,128)(4,1)S(1)} %compare_and_fusion, f32[128,2]{0,1:T(2,128)S(1)} %get-tuple-element.5), kind=kOutput, calls=%fused_computation.32 | convolution fusion | flops 201818112 | bytes 1312768 | tf_op jit(solution)/shard_map/hqk,khd->hqd/dot_general | solution.py:43
  42.0 0.7 %copy.53 = bf16[128,256]{1,0:T(8,128)(2,1)} copy(bf16[128,256]{0,1:T(8,128)(2,1)S(1)} %bitcast.166) | data formatting | bytes 131072 | tf_op jit(solution)/shard_map/convert_element_type | solution.py:86
  (12 shorter events, 0.1 us)
Async XLA Ops:
  0.0 9.9 %copy-start = (bf16[256,512]{1,0:T(8,128)(2,1)S(1)}, bf16[256,512]{1,0:T(8,128)(2,1)}, u32[]{:S(2)}) copy-start(bf16[256,512]{1,0:T(8,128)(2,1)} %param.5) | copy-start | bytes 786436
  6.2 3.4 %copy-start.1 = (bf16[128,384]{1,0:T(8,128)(2,1)S(1)}, bf16[128,384]{1,0:T(8,128)(2,1)}, u32[]{:S(2)}) copy-start(bf16[128,384]{1,0:T(8,128)(2,1)} %param.3) | copy-start | bytes 294916
  6.3 6.6 %collective-permute-start = (bf16[128,320]{0,1:T(8,128)(2,1)S(1)}, bf16[128,320]{0,1:T(8,128)(2,1)S(1)}, u32[]{:S(2)}, u32[]{:S(2)}) collective-permute-start(bf16[128,320]{0,1:T(8,128)(2,1)S(1)} %copy.39), channel_id=1, source_target_pairs={{0,4},{4,8},{8,12},{12,16},{16,20},{20,24},{24,28},{1,5},{5,9},{9,... | collective-permute-start | bytes 245768 | tf_op jit(solution)/shard_map/ppermute | solution.py:17
  12.9 6.6 %collective-permute-start.1 = (bf16[256,320]{0,1:T(8,128)(2,1)S(1)}, bf16[256,320]{0,1:T(8,128)(2,1)S(1)}, u32[]{:S(2)}, u32[]{:S(2)}) collective-permute-start(bf16[256,320]{0,1:T(8,128)(2,1)S(1)} %pad_maximum_fusion.1), channel_id=1, source_target_pairs={{0,8},{4,12},{8,16},{12,20},{16,24},{20,28},{1,9},{5,13},{9,17},{1... | collective-permute-start | bytes 491528 | tf_op jit(solution)/shard_map/ppermute | solution.py:17
  19.6 19.3 %collective-permute-start.2 = (bf16[512,320]{0,1:T(8,128)(2,1)S(1)}, bf16[512,320]{0,1:T(8,128)(2,1)S(1)}, u32[]{:S(2)}, u32[]{:S(2)}) collective-permute-start(bf16[512,320]{0,1:T(8,128)(2,1)S(1)} %pad_maximum_fusion), channel_id=1, source_target_pairs={{0,16},{4,20},{8,24},{12,28},{1,17},{5,21},{9,25},{13,29},{2,18},{... | collective-permute-start | bytes 983048 | tf_op jit(solution)/shard_map/ppermute | solution.py:17
where the time goes:
time: 42.9 us; the launch traced here: 42.7 us
  waiting for transfers between devices  23 us (54%)
  blocking collectives  6.16 us (14%)
  starting transfers between devices  5.73 us (13%)
  matrix products  4.62 us (11%)
  local copies, waits for them, and re-layouts  2.04 us (5%)
  other arithmetic  0.87 us (2%)
    ppermute x3, waiting for transfers between devices, from_behind(): return lax.ppermute(shard, axis, pairs)  23 us
    all_gather x1, blocking collectives, body(): gathered = lax.all_gather(latent, 'head', axis=0, tiled=True)  6.16 us
    ppermute x3, starting transfers between devices, from_behind(): return lax.ppermute(shard, axis, pairs)  5.73 us
    dot_general x4, matrix products, attend(): jnp.einsum('hqk,khd->hqd', rounded.astype(jnp.float32), key_value[:, :, N...  1.46 us
    dot_general x4, matrix products, attend(): jnp.einsum('qhd,khd->hqk', query_side, key_value[:, :, :NOPE], precision=...  1.25 us
    dot_general x4, matrix products, attend(): key_value = jnp.dot(key_latent, w_kv_up, preferred_element_type=jnp.float32)  0.97 us
    dot_general x4, matrix products, attend(): jnp.einsum('qhd,kd->hqk', query_rope, key_rope, preferred_element_type=jn...  0.94 us
  transfers between devices with their start and end apart: 3, of which 3 were waited for; matrix products, arithmetic and copies ran while one was open for 9% of the time, Pallas kernels for 0%

commit v1 on v0

--- a/solution.py
+++ b/solution.py
@@ -1,3 +1,4 @@
+import functools
 import math
 import jax
 import jax.numpy as jnp
@@ -9,6 +10,22 @@
 NOPE = 128
 VDIM = 128
 MASKED = -1e30
+
+
+def mark_tails_here(in_array, device_axis, dim_at):
+    k_all = jax.lax.axis_size(device_axis)
+    crops = [(to_i, (to_i + 1) % k_all) for to_i in range(k_all)]
+
+    def fill_flows(v_now):
+        if len(v_now) == k_all:
+            return v_now
+        return fill_flows([jax.lax.ppermute(v_now[0], device_axis, crops), *v_now])
+
+    now = jnp.concatenate(fill_flows([in_array]), dim_at)
+    return jnp.roll(now, (jax.lax.axis_index(device_axis) + 1) * in_array.shape[dim_at], dim_at)
+
+
+store_the_ranges = functools.partial(mark_tails_here, device_axis="head", dim_at=0)
 
 
 def from_behind(shard, axis, by):
@@ -93,7 +110,7 @@
     group_index = lax.axis_index("seq")
     query_pos = group_index * group_rows + lax.iota(jnp.int32, group_rows)
     setup, state = prepare(queries, query_pos, w_kv_up)
-    gathered = lax.all_gather(latent, "head", axis=0, tiled=True)
+    gathered = store_the_ranges(latent)
     state = attend(state, gathered, group_index * group_rows, setup)
     history = gathered
     span_groups = 1

time: 42.9 us -> 47.6 us (1.11)
  the two profiles are of different devices: /device:TPU:27 before, /device:TPU:24 now
where the time goes in v1:
time: 47.6 us; the launch traced here: 47.4 us
  waiting for transfers between devices  32.2 us (68%)
  starting transfers between devices  6.07 us (13%)
  matrix products  4.81 us (10%)
  local copies, waits for them, and re-layouts  3.17 us (7%)
  other arithmetic  0.88 us (2%)
    ppermute x3, waiting for transfers between devices, from_behind(): return lax.ppermute(shard, axis, pairs)  21.4 us
    ppermute x3, waiting for transfers between devices, fill_flows(): return fill_flows([jax.lax.ppermute(v_now[0], device_axis, crops), *v_now])  10.8 us
    ppermute x3, starting transfers between devices, from_behind(): return lax.ppermute(shard, axis, pairs)  6.01 us
    dot_general x4, matrix products, attend(): jnp.einsum('hqk,khd->hqd', rounded.astype(jnp.float32), key_value[:, :, N...  1.46 us
    dot_general x4, matrix products, attend(): jnp.einsum('qhd,khd->hqk', query_side, key_value[:, :, :NOPE], precision=...  1.23 us
    dot_general x4, matrix products, attend(): key_value = jnp.dot(key_latent, w_kv_up, preferred_element_type=jnp.float32)  1.07 us
    dot_general x4, matrix products, attend(): jnp.einsum('qhd,kd->hqk', query_rope, key_rope, preferred_element_type=jn...  1.04 us
    unnamed x6, local copies, waits for them, and re-layouts  1.03 us
  transfers between devices with their start and end apart: 6, of which 6 were waited for; matrix products, arithmetic and copies ran while one was open for 8% of the time, Pallas kernels for 0%

profile of v1, /device:TPU:24, one launch (start us, length us, event | category | flops | bytes accessed | tf_op | source)
XLA Modules:
  0.0 47.4 jit_solution(10608796393248915365)
XLA Ops:
  0.0 0.0 copy-start
  0.0 0.9 %copy.23 = bf16[32,320]{0,1:T(8,128)(2,1)S(1)} copy(bf16[32,320]{1,0:T(8,128)(2,1)} %param.4) | data formatting | bytes 40960 | tf_op args[1]
  0.9 0.1 collective-permute-start
  1.0 0.0 copy-start.1
  1.1 0.2 compare_and_fusion
  1.3 0.1 compare_and_fusion.2
  1.4 3.4 %collective-permute-done = bf16[32,320]{0,1:T(8,128)(2,1)S(1)} collective-permute-done((bf16[32,320]{0,1:T(8,128)(2,1)S(1)}, bf16[32,320]{0,1:T(8,128)(2,1)S(1)}, u32[]{:S(2)}, u32[]{:S(2)}) %collective-permute-start) | collective-permute-done | bytes 20512 | tf_op jit(solution)/shard_map/ppermute | solution.py:22
  4.8 0.0 collective-permute-start.1
  4.8 3.9 %collective-permute-done.1 = bf16[32,320]{0,1:T(8,128)(2,1)S(1)} collective-permute-done((bf16[32,320]{0,1:T(8,128)(2,1)S(1)}, bf16[32,320]{0,1:T(8,128)(2,1)S(1)}, u32[]{:S(2)}, u32[]{:S(2)}) %collective-permute-start.1) | collective-permute-done | bytes 20512 | tf_op jit(solution)/shard_map/ppermute | solution.py:22
  8.7 0.0 collective-permute-start.2
  8.7 0.1 compare_and_fusion.1
  8.8 0.0 copy-done.1
  8.9 0.1 copy.27
  9.0 3.6 %collective-permute-done.2 = bf16[32,320]{0,1:T(8,128)(2,1)S(1)} collective-permute-done((bf16[32,320]{0,1:T(8,128)(2,1)S(1)}, bf16[32,320]{0,1:T(8,128)(2,1)S(1)}, u32[]{:S(2)}, u32[]{:S(2)}) %collective-permute-start.2) | collective-permute-done | bytes 20512 | tf_op jit(solution)/shard_map/ppermute | solution.py:22
  12.6 0.2 concatenate.13
  12.8 0.1 constant_dynamic-slice_fusion
  12.9 3.4 %collective-permute-start.3 = (bf16[128,320]{0,1:T(8,128)(2,1)S(1)}, bf16[128,320]{0,1:T(8,128)(2,1)S(1)}, u32[]{:S(2)}, u32[]{:S(2)}) collective-permute-start(bf16[128,320]{0,1:T(8,128)(2,1)S(1)} %constant_dynamic-slice_fusion), channel_id=1, source_target_pairs={{0,4},{4,8},{8,12},{12,16},{16,20},{20,24},{24,28},{1,5},{5,9},{9,... | collective-permute-start | bytes 245768 | tf_op jit(solution)/shard_map/ppermute | solution.py:34
  16.4 0.0 copy-done
  16.4 0.3 fusion.53
  16.7 0.2 reshape.297
  16.8 0.1 fusion.87
  16.9 0.2 convolution_bitcast_fusion.9
  17.1 0.3 fusion.91
  17.4 2.7 %collective-permute-done.3 = bf16[128,320]{0,1:T(8,128)(2,1)S(1)} collective-permute-done((bf16[128,320]{0,1:T(8,128)(2,1)S(1)}, bf16[128,320]{0,1:T(8,128)(2,1)S(1)}, u32[]{:S(2)}, u32[]{:S(2)}) %collective-permute-start.3) | collective-permute-done | bytes 81952 | tf_op jit(solution)/shard_map/ppermute | solution.py:34
  20.2 1.3 %collective-permute-start.4 = (bf16[256,320]{0,1:T(8,128)(2,1)S(1)}, bf16[256,320]{0,1:T(8,128)(2,1)S(1)}, u32[]{:S(2)}, u32[]{:S(2)}) collective-permute-start(bf16[256,320]{0,1:T(8,128)(2,1)S(1)} %pad_maximum_fusion.1), channel_id=1, source_target_pairs={{0,8},{4,12},{8,16},{12,20},{16,24},{20,28},{1,9},{5,13},{9,17},{1... | collective-permute-start | bytes 491528 | tf_op jit(solution)/shard_map/ppermute | solution.py:34
  21.5 0.2 fusion.51
  21.7 0.2 reshape.299
  21.9 0.1 fusion.86
  22.0 0.2 convolution_bitcast_fusion.7
  22.2 0.2 fusion.90
  22.4 5.0 %collective-permute-done.4 = bf16[256,320]{0,1:T(8,128)(2,1)S(1)} collective-permute-done((bf16[256,320]{0,1:T(8,128)(2,1)S(1)}, bf16[256,320]{0,1:T(8,128)(2,1)S(1)}, u32[]{:S(2)}, u32[]{:S(2)}) %collective-permute-start.4) | collective-permute-done | bytes 163872 | tf_op jit(solution)/shard_map/ppermute | solution.py:34
  27.4 1.3 %collective-permute-start.5 = (bf16[512,320]{0,1:T(8,128)(2,1)S(1)}, bf16[512,320]{0,1:T(8,128)(2,1)S(1)}, u32[]{:S(2)}, u32[]{:S(2)}) collective-permute-start(bf16[512,320]{0,1:T(8,128)(2,1)S(1)} %pad_maximum_fusion), channel_id=1, source_target_pairs={{0,16},{4,20},{8,24},{12,28},{1,17},{5,21},{9,25},{13,29},{2,18},{... | collective-permute-start | bytes 983048 | tf_op jit(solution)/shard_map/ppermute | solution.py:34
  28.7 0.2 fusion.36
  29.0 0.3 reshape.300
  29.3 0.2 fusion.85
  29.5 0.2 convolution_bitcast_fusion.2
  29.8 0.2 fusion.89
  30.0 13.7 %collective-permute-done.5 = bf16[512,320]{0,1:T(8,128)(2,1)S(1)} collective-permute-done((bf16[512,320]{0,1:T(8,128)(2,1)S(1)}, bf16[512,320]{0,1:T(8,128)(2,1)S(1)}, u32[]{:S(2)}, u32[]{:S(2)}) %collective-permute-start.5) | collective-permute-done | bytes 327712 | tf_op jit(solution)/shard_map/ppermute | solution.py:34
  43.7 0.3 fusion.26
  44.0 0.6 %convolution_bitcast_fusion.1 = f32[2,128,512]{1,2,0:T(8,128)S(1)} fusion(f32[512,2,256]{0,2,1:T(8,128)S(1)} %bitcast.166, bf16[128,2,192]{0,2,1:T(8,128)(2,1)S(1)} %bitcast.164), kind=kOutput, calls=%fused_computation.2 | convolution fusion | flops 201326592 | bytes 1114112 | tf_op jit(solution)/shard_map/qhd,khd->hqk/dot_general | solution.py:47
  44.6 0.3 fusion.88
  44.9 0.1 fusion.23
  45.0 0.1 fusion.33
  45.2 0.3 fusion.12
  45.5 0.3 fusion.13
  45.8 0.4 fusion.9
  46.3 0.4 fusion.20
  46.7 0.7 %copy.39 = bf16[128,256]{1,0:T(8,128)(2,1)} copy(bf16[128,256]{0,1:T(8,128)(2,1)S(1)} %bitcast.168) | data formatting | bytes 131072 | tf_op jit(solution)/shard_map/convert_element_type | solution.py:103
  (13 shorter events, 0.2 us)
Async XLA Ops:
  0.0 16.4 %copy-start = (bf16[256,512]{1,0:T(8,128)(2,1)S(1)}, bf16[256,512]{1,0:T(8,128)(2,1)}, u32[]{:S(2)}) copy-start(bf16[256,512]{1,0:T(8,128)(2,1)} %param.5) | copy-start | bytes 786436
  0.9 3.9 %collective-permute-start = (bf16[32,320]{0,1:T(8,128)(2,1)S(1)}, bf16[32,320]{0,1:T(8,128)(2,1)S(1)}, u32[]{:S(2)}, u32[]{:S(2)}) collective-permute-start(bf16[32,320]{0,1:T(8,128)(2,1)S(1)} %copy.23), channel_id=1, source_target_pairs={{0,1},{1,2},{2,3},{3,0},{4,5},{5,6},{6,7},{7,4},{8,9},{9,10},{10,1... | collective-permute-start | bytes 61448 | tf_op jit(solution)/shard_map/ppermute | solution.py:22
  1.0 7.8 %copy-start.1 = (bf16[128,384]{1,0:T(8,128)(2,1)S(1)}, bf16[128,384]{1,0:T(8,128)(2,1)}, u32[]{:S(2)}) copy-start(bf16[128,384]{1,0:T(8,128)(2,1)} %param.3) | copy-start | bytes 294916
  4.8 3.9 %collective-permute-start.1 = (bf16[32,320]{0,1:T(8,128)(2,1)S(1)}, bf16[32,320]{0,1:T(8,128)(2,1)S(1)}, u32[]{:S(2)}, u32[]{:S(2)}) collective-permute-start(bf16[32,320]{0,1:T(8,128)(2,1)S(1)} %collective-permute-done), channel_id=1, source_target_pairs={{0,1},{1,2},{2,3},{3,0},{4,5},{5,6},{6,7},{7,4},{8,9},{9,10},{10,1... | collective-permute-start | bytes 61448 | tf_op jit(solution)/shard_map/ppermute | solution.py:22
  8.7 3.9 %collective-permute-start.2 = (bf16[32,320]{0,1:T(8,128)(2,1)S(1)}, bf16[32,320]{0,1:T(8,128)(2,1)S(1)}, u32[]{:S(2)}, u32[]{:S(2)}) collective-permute-start(bf16[32,320]{0,1:T(8,128)(2,1)S(1)} %collective-permute-done.1), channel_id=1, source_target_pairs={{0,1},{1,2},{2,3},{3,0},{4,5},{5,6},{6,7},{7,4},{8,9},{9,10},{10,1... | collective-permute-start | bytes 61448 | tf_op jit(solution)/shard_map/ppermute | solution.py:22
  12.9 7.2 %collective-permute-start.3 = (bf16[128,320]{0,1:T(8,128)(2,1)S(1)}, bf16[128,320]{0,1:T(8,128)(2,1)S(1)}, u32[]{:S(2)}, u32[]{:S(2)}) collective-permute-start(bf16[128,320]{0,1:T(8,128)(2,1)S(1)} %constant_dynamic-slice_fusion), channel_id=1, source_target_pairs={{0,4},{4,8},{8,12},{12,16},{16,20},{20,24},{24,28},{1,5},{5,9},{9,... | collective-permute-start | bytes 245768 | tf_op jit(solution)/shard_map/ppermute | solution.py:34
  20.2 7.2 %collective-permute-start.4 = (bf16[256,320]{0,1:T(8,128)(2,1)S(1)}, bf16[256,320]{0,1:T(8,128)(2,1)S(1)}, u32[]{:S(2)}, u32[]{:S(2)}) collective-permute-start(bf16[256,320]{0,1:T(8,128)(2,1)S(1)} %pad_maximum_fusion.1), channel_id=1, source_target_pairs={{0,8},{4,12},{8,16},{12,20},{16,24},{20,28},{1,9},{5,13},{9,17},{1... | collective-permute-start | bytes 491528 | tf_op jit(solution)/shard_map/ppermute | solution.py:34
  27.4 16.2 %collective-permute-start.5 = (bf16[512,320]{0,1:T(8,128)(2,1)S(1)}, bf16[512,320]{0,1:T(8,128)(2,1)S(1)}, u32[]{:S(2)}, u32[]{:S(2)}) collective-permute-start(bf16[512,320]{0,1:T(8,128)(2,1)S(1)} %pad_maximum_fusion), channel_id=1, source_target_pairs={{0,16},{4,20},{8,24},{12,28},{1,17},{5,21},{9,25},{13,29},{2,18},{... | collective-permute-start | bytes 983048 | tf_op jit(solution)/shard_map/ppermute | solution.py:34
